TPU v7x, 32 devices: a whole 2x2x4 slice. The times are simulated.
32 devices in a mesh: bx: 4 (over y, x), by: 8 (over z, core).
Axes of the slice: x: 2, y: 2, z: 4, core: 2. Of those that a mesh axis runs over, the one named last changes fastest.
Arguments:
- forcing: float32 [1216, 1024], P('by', 'bx'), may hold values from -20 to 20
- guess: float32 [1216, 1024], P('by', 'bx'), may hold values from -3 to 3
- shift: float32 [1216, 1024], P('by', 'bx'), may hold values from 0.05 to 2
- ocean_mask: int32 [1216, 1024], P('by', 'bx'), may hold values 0 or 1
Outputs:
- solution_field: float32 [1216, 1024], P('by', 'bx')
- residual: float32 [1216, 1024], P('by', 'bx')
- residual_norm: float32 [], replicated
All inputs are finite; a program needn't handle non-finite values. No bound on the sum of `ocean_mask` on one device may be relied on, other than what follows from the above.
Results may differ from a plain program's by a relative error of at most 0.00002.
Values sent between devices are 32-bit elements; how exact they have to be, the bound alone decides.
A program may use at most 64 MiB of HBM per device.

v0:
```python
import jax
import jax.numpy as jnp
from jax import lax
from jax.sharding import PartitionSpec as P

ITERS = 4


LOW_BOUND = 0.05
HIGH_BOUND = 14.5


def padded_2(block, sides, width):
    for axis, dim in sides:
        count = lax.axis_size(axis)
        forward = [(i, i + 1) for i in range(count - 1)]
        forward.append((count - 1, 0))
        backward = [(target, source) for source, target in forward]
        low = lax.ppermute(
            lax.slice_in_dim(block, block.shape[dim] - width, None, axis=dim), axis, forward
        )
        high = lax.ppermute(lax.slice_in_dim(block, 0, width, axis=dim), axis, backward)
        block = jnp.concatenate([low, block, high], axis=dim)
    return block


def stencil_padded(padded, shift, mask_f):
    center = padded[1:-1, 1:-1]
    sides = padded[2:, 1:-1] + padded[:-2, 1:-1] + padded[1:-1, 2:] + padded[1:-1, :-2]
    corners = padded[2:, 2:] + padded[2:, :-2] + padded[:-2, 2:] + padded[:-2, :-2]
    return mask_f * ((6.0 + shift) * center - sides - 0.5 * corners)


def crop_cycle(values, cycle):
    return values[cycle : values.shape[0] - cycle, cycle : values.shape[1] - cycle]


def local_stencil(values, shift_full, mask_full):
    cycle = (shift_full.shape[0] - values.shape[0]) // 2 + 1
    return stencil_padded(values, crop_cycle(shift_full, cycle), crop_cycle(mask_full, cycle))


def deep_inputs(forcing, guess, shift, mask_f):
    rows, cols = forcing.shape
    depth = ITERS + 1
    stacked = jnp.stack([forcing, guess, shift, mask_f])
    padded = padded_2(stacked, (("bx", 2), ("by", 1)), depth)
    top_rows = stacked[:, rows - depth :, :]
    whole_top = lax.all_gather(top_rows, "bx", axis=2, tiled=True)
    flipped = whole_top[:, ::-1, ::-1]
    extended = jnp.concatenate([flipped[:, :, -depth:], flipped, flipped[:, :, :depth]], axis=2)
    ghost = lax.dynamic_slice_in_dim(extended, lax.axis_index("bx") * cols, cols + 2 * depth, 2)
    row_index = lax.axis_index("by")
    upper_rows = jnp.where(row_index == lax.axis_size("by") - 1, ghost, padded[:, rows + depth :])
    lower_rows = jnp.where(row_index == 0, jnp.zeros_like(ghost), padded[:, :depth])
    return jnp.concatenate([lower_rows, padded[:, depth : rows + depth], upper_rows], axis=1)


def pair_add(first, second):
    total = first[0] + second[0]
    backed = total - first[0]
    error = first[0] - (total - backed) + (second[0] - backed)
    error = error + first[1] + second[1]
    upper = total + error
    lower = error - (upper - total)
    return (upper, lower)


def tree_total(uppers, lowers):
    while uppers.shape[0] > 1:
        if uppers.shape[0] % 2 == 1:
            uppers = jnp.concatenate([uppers, jnp.zeros((1,), uppers.dtype)])
            lowers = jnp.concatenate([lowers, jnp.zeros((1,), lowers.dtype)])
        uppers, lowers = pair_add((uppers[0::2], lowers[0::2]), (uppers[1::2], lowers[1::2]))
    return (uppers[0], lowers[0])


def per_device(forcing, guess, shift, ocean_mask):
    mask_f = ocean_mask.astype(jnp.float32)
    theta = (HIGH_BOUND + LOW_BOUND) / 2.0
    delta = (HIGH_BOUND - LOW_BOUND) / 2.0
    sigma = theta / delta
    rho = 1.0 / sigma
    full = deep_inputs(forcing, guess, shift, mask_f)
    forcing_full = full[0]
    guess_full = full[1]
    shift_full = full[2]
    mask_full = full[3]
    iterate = mask_full * guess_full
    resid = crop_cycle(mask_full * forcing_full, 1) - local_stencil(iterate, shift_full, mask_full)
    direction = resid / theta
    iterate = crop_cycle(iterate, 1)
    for sweep in range(ITERS):
        iterate = iterate + direction
        image = local_stencil(direction, shift_full, mask_full)
        resid = crop_cycle(resid, 1) - image
        rho_next = 1.0 / (2.0 * sigma - rho)
        direction = rho_next * rho * crop_cycle(direction, 1) + 2.0 * rho_next / delta * resid
        rho = rho_next
        iterate = crop_cycle(iterate, 1)
    row_sums = jnp.sum(resid * resid, axis=1)
    upper, lower = tree_total(row_sums, jnp.zeros_like(row_sums))
    all_upper, all_lower = (
        lax.all_gather(upper[None], ("bx", "by"), axis=0, tiled=True),
        lax.all_gather(lower[None], ("bx", "by"), axis=0, tiled=True),
    )
    upper, lower = tree_total(all_upper, all_lower)
    grid_cells = resid.shape[0] * lax.axis_size("by") * resid.shape[1] * lax.axis_size("bx")
    norm_value = jnp.sqrt((upper + lower) / grid_cells)
    return (iterate, resid, norm_value)


def solution(mesh):
    in_specs = (P("by", "bx"), P("by", "bx"), P("by", "bx"), P("by", "bx"))
    out_specs = (P("by", "bx"), P("by", "bx"), P())
    return jax.shard_map(
        per_device, mesh=mesh, in_specs=in_specs, out_specs=out_specs, check_vma=False
    )
```

profile of v0, /device:TPU:0, one launch (start us, length us, event | category | flops | bytes accessed | tf_op | source)
XLA Modules:
  0.0 87.8 jit_solution(3005025311582672974)
XLA Ops:
  0.7 1.0 %convert_bitcast_fusion = f32[1,152,256]{2,1,0:T(8,128)S(1)} fusion(s32[152,256]{1,0:T(8,128)} %param.7), kind=kLoop, calls=%fused_computation.81 | loop fusion | flops 38912 | bytes 311296 | tf_op jit(solution)/shard_map/stack | solution.py:46
  1.7 1.0 %pad_maximum_fusion.1 = f32[4,152,256]{2,1,0:T(8,128)S(1)} fusion(f32[1,152,256]{2,1,0:T(8,128)S(1)} %convert_bitcast_fusion, f32[1,152,256]{2,1,0:T(8,128)S(1)} %bitcast.18, f32[1,152,256]{2,1,0:T(8,128)S(1)} %bitcast.22, f32[1,152,256]{2,1,0:T(8,128)} %bitcast.26), kind=kLoop, calls=%fused_computation.1 | loop fusion | flops 466944 | bytes 1245184 | tf_op jit(solution)/shard_map/stack | solution.py:46
  2.7 0.1 fusion.38
  2.8 3.0 %collective-permute-start = (f32[4,152,5]{2,1,0:T(8,128)S(1)}, f32[4,152,5]{2,1,0:T(8,128)S(1)}, u32[]{:S(2)}, u32[]{:S(2)}) collective-permute-start(f32[4,152,5]{2,1,0:T(8,128)S(1)} %get-tuple-element.62), channel_id=1, source_target_pairs={{0,8},{8,16},{16,24},{24,0},{1,9},{9,17},{17,25},{25,1},{2,10},{10... | collective-permute-start | bytes 36488 | tf_op jit(solution)/shard_map/ppermute | solution.py:19
  5.8 1.0 %collective-permute-start.1 = (f32[4,152,5]{2,1,0:T(8,128)S(1)}, f32[4,152,5]{2,1,0:T(8,128)S(1)}, u32[]{:S(2)}, u32[]{:S(2)}) collective-permute-start(f32[4,152,5]{2,1,0:T(8,128)S(1)} %get-tuple-element.63), channel_id=1, source_target_pairs={{8,0},{16,8},{24,16},{0,24},{9,1},{17,9},{25,17},{1,25},{10,2},{18... | collective-permute-start | bytes 36488 | tf_op jit(solution)/shard_map/ppermute | solution.py:22
  6.9 17.0 %all_gather.9 = f32[4,5,1024]{2,1,0:T(8,128)S(1)} all-gather(f32[4,5,256]{2,1,0:T(8,128)S(1)} %pad_maximum_fusion.8), channel_id=1, replica_groups=mesh['bx'=4,'by'=8] {'bx'}, dimensions={2}, use_global_device_ids=true | all-gather | bytes 102400 | tf_op jit(solution)/shard_map/all_gather | solution.py:49
  23.9 0.1 pad_maximum_fusion.7
  24.1 0.7 rev.3
  25.0 0.1 concatenate.28
  25.1 3.6 %collective-permute-start.3 = (f32[4,5,266]{2,1,0:T(8,128)S(1)}, f32[4,5,266]{2,1,0:T(8,128)S(1)}, u32[]{:S(2)}, u32[]{:S(2)}) collective-permute-start(f32[4,5,266]{2,1,0:T(8,128)S(1)} %get-tuple-element.58), channel_id=1, source_target_pairs={{1,0},{2,1},{3,2},{4,3},{5,4},{6,5},{7,6},{0,7},{9,8},{10,9},{11,1... | collective-permute-start | bytes 63848 | tf_op jit(solution)/shard_map/ppermute | solution.py:22
  28.7 0.6 collective-permute-done.2
  29.3 1.1 %collective-permute-done.3 = f32[4,5,266]{2,1,0:T(8,128)S(1)} collective-permute-done((f32[4,5,266]{2,1,0:T(8,128)S(1)}, f32[4,5,266]{2,1,0:T(8,128)S(1)}, u32[]{:S(2)}, u32[]{:S(2)}) %collective-permute-start.3) | collective-permute-done | bytes 21312 | tf_op jit(solution)/shard_map/ppermute | solution.py:22
  30.5 0.4 pad_maximum_fusion
  31.1 0.1 slice.570
  31.2 0.7 broadcast_multiply_fusion
  31.9 0.1 slice.571
  32.0 0.6 multiply_add_fusion.2
  32.6 0.1 slice.572
  32.8 0.6 multiply_add_fusion.1
  33.4 0.6 multiply_add_fusion
  34.1 1.4 %multiply_reduce_fusion = (f32[152]{0:T(256)S(1)}, f32[152,256]{1,0:T(8,128)}, f32[152,256]{1,0:T(8,128)}) fusion(f32[154,258]{1,0:T(8,128)S(1)} %get-tuple-element.49, f32[162,266]{1,0:T(8,128)S(1)} %get-tuple-element.60, f32[162,266]{1,0:T(8,128)S(1)} %get-tuple-element.59, f32[154,258]{1,0:T(8,128)S(1)} %get-tuple-element.50, ...), kind=kLoop, calls=%fused_computation.80 | loop fusion | flops 739176 | bytes 2802272 | tf_op jit(solution)/shard_map/reduce_sum | solution.py:101
  35.5 0.2 slice.471
  35.6 0.2 slice.470
  35.8 0.1 slice.475
  36.0 0.1 slice.474
  36.1 0.1 slice.473
  36.2 0.1 slice.472
  36.4 0.1 slice.479
  36.5 0.1 slice.478
  36.6 0.1 slice.477
  36.7 0.1 slice.476
  36.9 0.1 slice.483
  37.1 0.1 slice.481
  37.2 0.1 slice.480
  37.9 0.1 slice.489
  38.1 0.1 slice.491
  38.4 0.1 slice.493
  38.7 0.1 slice.495
  38.9 0.6 add_dynamic-update-slice_fusion
  39.5 0.8 subtract_dynamic-update-slice_fusion
  40.3 38.8 %all-reduce.2 = (f32[32]{0:T(128)S(1)}, f32[32]{0:T(128)S(1)}) all-reduce(f32[32]{0:T(128)S(1)} %get-tuple-element.72, f32[32]{0:T(128)S(1)} %subtract_dynamic-update-slice_fusion), channel_id=1, replica_groups=mesh['bx'=4,'by'=8] {'bx','by'}, use_global_device_ids=true, to_apply=%add | all-reduce | flops 64 | bytes 512
  79.2 0.1 slice.500
  79.3 0.1 slice.501
  79.4 0.1 slice.502
  79.5 0.1 slice.503
  79.9 0.1 slice.504
  80.8 0.6 fusion.41
  84.1 0.6 fusion.40
  (66 shorter events, 3.1 us)
Async XLA Ops:
  0.6 1.0 %copy-start = (f32[152,256]{1,0:T(8,128)S(1)}, f32[152,256]{1,0:T(8,128)}, u32[]{:S(2)}) copy-start(f32[152,256]{1,0:T(8,128)} %param.6) | copy-start | bytes 466948
  0.6 1.1 %copy-start.1 = (f32[152,256]{1,0:T(8,128)S(1)}, f32[152,256]{1,0:T(8,128)}, u32[]{:S(2)}) copy-start(f32[152,256]{1,0:T(8,128)} %param.5) | copy-start | bytes 466948
  2.7 4.2 %copy-start.2 = (f32[152,256]{1,0:T(8,128)S(1)}, f32[152,256]{1,0:T(8,128)}, u32[]{:S(2)}) copy-start(f32[152,256]{1,0:T(8,128)} %param.4) | copy-start | bytes 466948
  2.8 21.0 %collective-permute-start = (f32[4,152,5]{2,1,0:T(8,128)S(1)}, f32[4,152,5]{2,1,0:T(8,128)S(1)}, u32[]{:S(2)}, u32[]{:S(2)}) collective-permute-start(f32[4,152,5]{2,1,0:T(8,128)S(1)} %get-tuple-element.62), channel_id=1, source_target_pairs={{0,8},{8,16},{16,24},{24,0},{1,9},{9,17},{17,25},{25,1},{2,10},{10... | collective-permute-start | bytes 36488 | tf_op jit(solution)/shard_map/ppermute | solution.py:19
  5.8 18.0 %collective-permute-start.1 = (f32[4,152,5]{2,1,0:T(8,128)S(1)}, f32[4,152,5]{2,1,0:T(8,128)S(1)}, u32[]{:S(2)}, u32[]{:S(2)}) collective-permute-start(f32[4,152,5]{2,1,0:T(8,128)S(1)} %get-tuple-element.63), channel_id=1, source_target_pairs={{8,0},{16,8},{24,16},{0,24},{9,1},{17,9},{25,17},{1,25},{10,2},{18... | collective-permute-start | bytes 36488 | tf_op jit(solution)/shard_map/ppermute | solution.py:22
  24.0 5.4 %collective-permute-start.2 = (f32[4,5,266]{2,1,0:T(8,128)S(1)}, f32[4,5,266]{2,1,0:T(8,128)S(1)}, u32[]{:S(2)}, u32[]{:S(2)}) collective-permute-start(f32[4,5,266]{2,1,0:T(8,128)S(1)} %get-tuple-element.57), channel_id=1, source_target_pairs={{0,1},{1,2},{2,3},{3,4},{4,5},{5,6},{6,7},{7,0},{8,9},{9,10},{10,1... | collective-permute-start | bytes 63848 | tf_op jit(solution)/shard_map/ppermute | solution.py:19
  25.1 5.3 %collective-permute-start.3 = (f32[4,5,266]{2,1,0:T(8,128)S(1)}, f32[4,5,266]{2,1,0:T(8,128)S(1)}, u32[]{:S(2)}, u32[]{:S(2)}) collective-permute-start(f32[4,5,266]{2,1,0:T(8,128)S(1)} %get-tuple-element.58), channel_id=1, source_target_pairs={{1,0},{2,1},{3,2},{4,3},{5,4},{6,5},{7,6},{0,7},{9,8},{10,9},{11,1... | collective-permute-start | bytes 63848 | tf_op jit(solution)/shard_map/ppermute | solution.py:22
where the time goes:
time: 88.3 us; the launch traced here: 87.8 us
  blocking collectives  55.8 us (63%)
  other arithmetic  8.6 us (10%)
  starting transfers between devices  7.68 us (9%)
  local copies, waits for them, and re-layouts  7.26 us (8%)
  between operations  6.75 us (8%)
  waiting for transfers between devices  1.75 us (2%)
    unnamed x1, blocking collectives  38.8 us
    all_gather x1, blocking collectives, deep_inputs(): whole_top = lax.all_gather(top_rows, 'bx', axis=2, tiled=True)  17 us
    ppermute x2, starting transfers between devices, padded_2(): lax.ppermute(lax.slice_in_dim(block, 0, width, axis=dim), axis, backward)  4.6 us
    ppermute x2, starting transfers between devices, padded_2(): lax.ppermute(lax.slice_in_dim(block, block.shape[dim] - width, None, axis...  3.07 us
    add x3, other arithmetic, per_device(): rho_next * rho * crop_cycle(direction, 1) + 2.0 * rho_next / delta * resid  1.94 us
    another operation x2, other arithmetic, deep_inputs(): stacked = jnp.stack([forcing, guess, shift, mask_f])  1.93 us
    slice x12, local copies, waits for them, and re-layouts, tree_total(): uppers[1::2]  1.78 us
  transfers between devices with their start and end apart: 4, of which 2 were waited for; matrix products, arithmetic and copies ran while one was open for 1% of the time, Pallas kernels for 0%

commit v1 on v0

v1 whole, which is shorter than its diff:
```python
import functools

import jax
import jax.numpy as jnp
from jax import lax
from jax.experimental import pallas as pl
from jax.experimental.pallas import tpu as pltpu
from jax.sharding import PartitionSpec as P

ITERS = 4
LOW_BOUND = 0.05
HIGH_BOUND = 14.5

EDGE = 8
LANES = 128
FIELDS = 4
SW, SE, NW, NE = 0, 1, 2, 3
MESH_ID = pl.DeviceIdType.MESH


def pair_add(first, second):
    total = first[0] + second[0]
    backed = total - first[0]
    error = first[0] - (total - backed) + (second[0] - backed)
    error = error + first[1] + second[1]
    upper = total + error
    lower = error - (upper - total)
    return (upper, lower)


def pair_tree(pairs):
    while len(pairs) > 1:
        merged = [pair_add(pairs[i], pairs[i + 1]) for i in range(0, len(pairs) - 1, 2)]
        if len(pairs) % 2 == 1:
            merged.append(pairs[-1])
        pairs = merged
    return pairs[0]


def flip_tile(tile):
    lane = lax.broadcasted_iota(jnp.int32, tile.shape, 1)
    row = lax.broadcasted_iota(jnp.int32, tile.shape, 0)
    tile = jnp.take_along_axis(tile, tile.shape[1] - 1 - lane, axis=1)
    return jnp.take_along_axis(tile, tile.shape[0] - 1 - row, axis=0)


def turn(tile, shift):
    shift = shift % LANES
    return tile if shift == 0 else pltpu.roll(tile, shift, 1)


def kernel(
    sizes,
    f_in, g_in, s_in, m_in,
    x_out, r_out, norm_out,
    ext, ext_m, mask, flip_f, flip_m, pack, came, corner, flip_c, x_buf, r_buf, part, parts,
    load_sem, send_sem, recv_sem, part_send, part_recv, own_sem, out_sem,
):
    nbx, nby, rows, cols = sizes
    n = nbx * nby
    bx, by = lax.axis_index("bx"), lax.axis_index("by")
    me = bx * nby + by
    fold = by == nby - 1
    bottom = by == 0
    east, west = lax.rem(bx + 1, nbx), lax.rem(bx + nbx - 1, nbx)
    low, high = EDGE, EDGE + rows
    whole = high + EDGE
    tiles = rows // 8
    chunks = LANES // (FIELDS * EDGE)
    per_chunk = -(-tiles // chunks)
    top_chunk, top_slot = divmod(tiles - 1, per_chunk)
    top = pl.ds(8 * top_slot, 8)
    lane = lax.broadcasted_iota(jnp.int32, (8, LANES), 1)

    loads = [
        pltpu.make_async_copy(source, ext.at[k, pl.ds(low, rows), pl.ds(0, cols)], load_sem.at[k])
        for k, source in enumerate((f_in, g_in, s_in))
    ]
    loads.append(pltpu.make_async_copy(m_in, ext_m.at[pl.ds(low, rows), :], load_sem.at[3]))
    for copy in loads:
        copy.start()

    barrier = pltpu.get_barrier_semaphore()

    def greet(k, carry):
        other = lax.rem(me + k, n)
        pl.semaphore_signal(
            barrier, inc=1, device_id=(other // nby, lax.rem(other, nby)), device_id_type=MESH_ID
        )
        return carry

    lax.fori_loop(1, n, greet, 0)

    for copy in loads:
        copy.wait()

    packed = [[jnp.zeros((8, LANES), jnp.float32)] * per_chunk for _ in range(2)]
    for t in range(tiles):
        chunk, slot = divmod(t, per_chunk)
        here = pl.ds(low + 8 * t, 8)
        for f in range(FIELDS):
            group = chunk * FIELDS + f
            if f < 3:
                left, right = ext[f, here, :LANES], ext[f, here, cols - LANES : cols]
            else:
                left = ext_m[here, :LANES].astype(jnp.float32)
                right = ext_m[here, cols - LANES :].astype(jnp.float32)
            keep = lane // EDGE == group
            packed[0][slot] = jnp.where(keep, turn(left, EDGE * group), packed[0][slot])
            packed[1][slot] = jnp.where(keep, turn(right, EDGE * group + EDGE), packed[1][slot])
    for side in range(2):
        for slot in range(per_chunk):
            pack[side, 8 * slot : 8 * slot + 8, :] = packed[side][slot]

    @pl.when(fold)
    def _():
        last = pl.ds(high - 8, 8)
        count = cols // LANES
        for j in range(count):
            src = pl.ds((count - 1 - j) * LANES, LANES)
            dst = pl.ds(j * LANES, LANES)
            for f in range(3):
                flip_f[f, :, dst] = flip_tile(ext[f, last, src])
            flip_m[:, dst] = flip_tile(ext_m[last, src])
        for side in range(2):
            flip_c[side] = flip_tile(pack[side, top, :])

    @pl.when(bottom)
    def _():
        ext[:, 0:EDGE, 0:cols] = jnp.zeros((3, EDGE, cols), jnp.float32)
        ext_m[0:EDGE, :] = jnp.zeros((EDGE, cols), jnp.int32)
        corner[SW] = jnp.zeros((8, LANES), jnp.float32)
        corner[SE] = jnp.zeros((8, LANES), jnp.float32)

    pl.semaphore_wait(barrier, n - 1)

    south_rows, north_rows = pl.ds(0, EDGE), pl.ds(high, EDGE)
    body = pl.ds(0, cols)

    def send(src, dst, slot, order, target):
        return pltpu.make_async_remote_copy(
            src_ref=src, dst_ref=dst, send_sem=send_sem.at[order], recv_sem=recv_sem.at[slot],
            device_id=target, device_id_type=MESH_ID,
        )

    to_west = send(pack.at[0], came.at[0], 8, 0, (west, by))
    to_east = send(pack.at[1], came.at[1], 9, 1, (east, by))

    south = lax.max(by - 1, 0)
    first_rows = pl.ds(low, EDGE)
    last_rows = pl.ds(high - EDGE, EDGE)
    to_south = [
        send(pack.at[0, pl.ds(0, 8), :], corner.at[NE], NE, 4, (west, south)),
        send(pack.at[1, pl.ds(0, 8), :], corner.at[NW], NW, 5, (east, south)),
        send(ext.at[:, first_rows, body], ext.at[:, north_rows, body], 6, 2, (bx, south)),
        send(ext_m.at[first_rows, :], ext_m.at[north_rows, :], 7, 3, (bx, south)),
    ]
    north = lax.min(by + 1, nby - 1)
    to_north = [
        send(pack.at[0, top, :], corner.at[SE], SE, 8, (west, north)),
        send(pack.at[1, top, :], corner.at[SW], SW, 9, (east, north)),
        send(ext.at[:, last_rows, body], ext.at[:, south_rows, body], 4, 6, (bx, north)),
        send(ext_m.at[last_rows, :], ext_m.at[south_rows, :], 5, 7, (bx, north)),
    ]
    partner = nbx - 1 - bx
    partner_east = lax.rem(partner + 1, nbx)
    partner_west = lax.rem(partner + nbx - 1, nbx)
    over_fold = [
        send(flip_f, ext.at[:, north_rows, body], 6, 6, (partner, by)),
        send(flip_m, ext_m.at[north_rows, :], 7, 7, (partner, by)),
    ]
    fold_corners = [
        (send(flip_c.at[0], corner.at[NW], NW, 8, (partner_east, by)),
         pltpu.make_async_copy(flip_c.at[0], corner.at[NW], recv_sem.at[NW]), partner_east),
        (send(flip_c.at[1], corner.at[NE], NE, 9, (partner_west, by)),
         pltpu.make_async_copy(flip_c.at[1], corner.at[NE], recv_sem.at[NE]), partner_west),
    ]

    @pl.when(jnp.logical_not(bottom))
    def _():
        for copy in to_south:
            copy.start()

    @pl.when(jnp.logical_not(fold))
    def _():
        for copy in to_north:
            copy.start()

    @pl.when(fold)
    def _():
        for remote, local, target in fold_corners:
            pl.when(target != bx)(remote.start)
            pl.when(target == bx)(local.start)
        for copy in over_fold:
            copy.start()

    to_west.start()
    to_east.start()

    to_west.wait_recv()
    to_east.wait_recv()

    for t in range(tiles):
        chunk, slot = divmod(t, per_chunk)
        here = pl.ds(low + 8 * t, 8)
        from_east = came[0, 8 * slot : 8 * slot + 8, :]
        from_west = came[1, 8 * slot : 8 * slot + 8, :]
        for f in range(FIELDS):
            group = chunk * FIELDS + f
            value = jnp.where(
                lane < EDGE,
                turn(from_east, -EDGE * group),
                jnp.where(lane >= LANES - EDGE, turn(from_west, -EDGE - EDGE * group), 0.0),
            )
            if f < 3:
                ext[f, here, cols:] = value
            else:
                mask[here, cols:] = value

    @pl.when(jnp.logical_not(bottom))
    def _():
        to_north[0].wait_recv()
        to_north[1].wait_recv()
        to_north[2].wait_recv()
        to_north[3].wait_recv()

    for copy in to_south:
        copy.wait_recv()

    corners = [corner[k] for k in range(4)]
    for f in range(FIELDS):
        group = top_chunk * FIELDS + f
        flipped = LANES // EDGE - 1 - group
        south_tile = jnp.where(
            lane < EDGE,
            turn(corners[SE], -EDGE * group),
            jnp.where(lane >= LANES - EDGE, turn(corners[SW], -EDGE - EDGE * group), 0.0),
        )
        north_east = jnp.where(
            fold, turn(corners[NE], -EDGE * flipped), turn(corners[NE], -EDGE * f)
        )
        north_west = jnp.where(
            fold, turn(corners[NW], -EDGE - EDGE * flipped), turn(corners[NW], -EDGE - EDGE * f)
        )
        north_tile = jnp.where(
            lane < EDGE, north_east, jnp.where(lane >= LANES - EDGE, north_west, 0.0)
        )
        if f < 3:
            ext[f, south_rows, cols:] = south_tile
            ext[f, north_rows, cols:] = north_tile
        else:
            mask[south_rows, cols:] = south_tile
            mask[north_rows, cols:] = north_tile
    mask[:, :cols] = ext_m[...].astype(jnp.float32)

    width = cols + LANES
    theta = (HIGH_BOUND + LOW_BOUND) / 2.0
    delta = (HIGH_BOUND - LOW_BOUND) / 2.0
    sigma = theta / delta
    rho = 1.0 / sigma

    wet = mask[...]
    diagonal = wet * (6.0 + ext[2])

    def apply(values):
        across = pltpu.roll(values, 1, 1) + pltpu.roll(values, width - 1, 1)
        column = values + 0.5 * across
        around = across + pltpu.roll(column, 1, 0) + pltpu.roll(column, whole - 1, 0)
        return diagonal * values - wet * around

    iterate = wet * ext[1]
    resid = wet * ext[0] - apply(iterate)
    direction = resid * (1.0 / theta)
    for sweep in range(ITERS):
        iterate = iterate + direction
        resid = resid - apply(direction)
        rho_next = 1.0 / (2.0 * sigma - rho)
        if sweep < ITERS - 1:
            direction = (rho_next * rho) * direction + (2.0 * rho_next / delta) * resid
        rho = rho_next

    final = resid[low:high, :cols]
    x_buf[...] = iterate[low:high, :cols]
    r_buf[...] = final
    out_x = pltpu.make_async_copy(x_buf, x_out, out_sem.at[0])
    out_r = pltpu.make_async_copy(r_buf, r_out, out_sem.at[1])
    out_x.start()
    out_r.start()

    square = final * final
    row_sums = jnp.sum(square, axis=1, keepdims=True)
    zero = jnp.zeros((8, 1), jnp.float32)
    pair = pair_tree([(row_sums[8 * t : 8 * t + 8], zero) for t in range(tiles)])
    pair = [jnp.broadcast_to(word, (8, LANES)) for word in pair]
    for step in (4, 2, 1):
        pair = pair_add(pair, [pltpu.roll(word, step, 0) for word in pair])
    part[...] = jnp.where(lane < LANES // 2, pair[0], pair[1])[0:1]

    def share(k):
        other = lax.rem(me + k, n)
        return pltpu.make_async_remote_copy(
            src_ref=part, dst_ref=parts.at[me], send_sem=part_send.at[k], recv_sem=part_recv.at[me],
            device_id=(other // nby, lax.rem(other, nby)), device_id_type=MESH_ID,
        )

    def begin(k, carry):
        share(k).start()
        return carry

    lax.fori_loop(1, n, begin, 0)
    parts[me] = part[...]

    to_west.wait_send()
    to_east.wait_send()

    @pl.when(jnp.logical_not(bottom))
    def _():
        for copy in to_south:
            copy.wait_send()

    @pl.when(jnp.logical_not(fold))
    def _():
        for copy in to_north:
            copy.wait_send()

    @pl.when(fold)
    def _():
        for remote, local, target in fold_corners:
            pl.when(target != bx)(remote.wait_send)
        for copy in over_fold:
            copy.wait_send()

    def finish(k, carry):
        share(k).wait_send()
        source = lax.rem(me + k, n)
        pltpu.make_async_copy(part, parts.at[source], part_recv.at[source]).wait()
        return carry

    lax.fori_loop(1, n, finish, 0)

    def words(i):
        row = parts[i]
        return row, pltpu.roll(row, LANES // 2, 1)

    upper, lower = pair_tree([words(i) for i in range(n)])
    norm_out[...] = jnp.sqrt((upper + lower) / (rows * cols * n))[:, 0:1]
    out_x.wait()
    out_r.wait()


def per_device(sizes, forcing, guess, shift, ocean_mask):
    nbx, nby, rows, cols = sizes
    n = nbx * nby
    whole, width = rows + 2 * EDGE, cols + LANES
    chunks = LANES // (FIELDS * EDGE)
    pack_rows = 8 * -(-(rows // 8) // chunks)
    f32 = jnp.float32
    hbm = pl.BlockSpec(memory_space=pl.ANY)
    x, r, norm = pl.pallas_call(
        functools.partial(kernel, sizes),
        out_shape=(
            jax.ShapeDtypeStruct((rows, cols), f32),
            jax.ShapeDtypeStruct((rows, cols), f32),
            jax.ShapeDtypeStruct((1, 1), f32),
        ),
        in_specs=[hbm] * 4,
        out_specs=(hbm, hbm, pl.BlockSpec(memory_space=pltpu.VMEM)),
        scratch_shapes=[
            pltpu.VMEM((3, whole, width), f32),
            pltpu.VMEM((whole, cols), jnp.int32),
            pltpu.VMEM((whole, width), f32),
            pltpu.VMEM((3, EDGE, cols), f32),
            pltpu.VMEM((EDGE, cols), jnp.int32),
            pltpu.VMEM((2, pack_rows, LANES), f32),
            pltpu.VMEM((2, pack_rows, LANES), f32),
            pltpu.VMEM((4, 8, LANES), f32),
            pltpu.VMEM((2, 8, LANES), f32),
            pltpu.VMEM((rows, cols), f32),
            pltpu.VMEM((rows, cols), f32),
            pltpu.VMEM((1, LANES), f32),
            pltpu.VMEM((n, 1, LANES), f32),
            pltpu.SemaphoreType.DMA((4,)),
            pltpu.SemaphoreType.DMA((10,)),
            pltpu.SemaphoreType.DMA((10,)),
            pltpu.SemaphoreType.DMA((n,)),
            pltpu.SemaphoreType.DMA((n,)),
            pltpu.SemaphoreType.DMA((1,)),
            pltpu.SemaphoreType.DMA((2,)),
        ],
        compiler_params=pltpu.CompilerParams(collective_id=0, has_side_effects=True),
        name="chebyshev",
    )(forcing, guess, shift, ocean_mask)
    return x, r, norm.reshape(())


def solution(mesh):
    spec = P("by", "bx")
    nbx, nby = mesh.shape["bx"], mesh.shape["by"]

    def run(forcing, guess, shift, ocean_mask):
        sizes = (nbx, nby, forcing.shape[0] // nby, forcing.shape[1] // nbx)
        return jax.shard_map(
            functools.partial(per_device, sizes),
            mesh=mesh,
            in_specs=(spec,) * 4,
            out_specs=(spec, spec, P()),
            check_vma=False,
        )(forcing, guess, shift, ocean_mask)

    return run
```

time: 88.3 us -> 22 us (0.25)
  blocking collectives: 55.8 us -> 0 us
  Pallas kernels: 0 us -> 17.1 us
  other arithmetic: 8.6 us -> 0 us
  starting transfers between devices: 7.68 us -> 0 us
  local copies, waits for them, and re-layouts: 7.26 us -> 2.29 us
  between operations: 6.75 us -> 2.4 us
  waiting for transfers between devices: 1.75 us -> 0 us
    unnamed x1 -> x0, blocking collectives: 38.8 us -> none
    pallas_call x0 -> x1, Pallas kernels: none -> 17.1 us  [per_device(): pl.pallas_call(functools.partial(kernel, sizes), out_shape=(jax.ShapeDtyp...]
    all_gather x1 -> x0, blocking collectives: 17 us -> none  [deep_inputs(): whole_top = lax.all_gather(top_rows, 'bx', axis=2, tiled=True)]
    ppermute x4 -> x0, starting transfers between devices: 7.68 us -> none  [the longest x2 4.6 us: padded_2(): lax.ppermute(lax.slice_in_dim(block, 0, width, axis=dim), axis, backward)]
    slice x51 -> x0, local copies, waits for them, and re-layouts: 6.32 us -> none  [the longest x12 1.78 us: tree_total(): uppers[1::2]]
    unnamed x8 -> x4, local copies, waits for them, and re-layouts: 0.08 us -> 2.29 us
    add x14 -> x0, other arithmetic: 2.08 us -> none  [the longest x3 1.94 us: per_device(): rho_next * rho * crop_cycle(direction, 1) + 2.0 * rho_next / delta * resid]
    another operation x2 -> x0, other arithmetic: 1.93 us -> none  [deep_inputs(): stacked = jnp.stack([forcing, guess, shift, mask_f])]
  transfers between devices with their start and end apart: 4 -> 0, of which waited for: 2 -> 0; matrix products, arithmetic and copies ran while one was open for 1% -> 0% of each run, Pallas kernels for 0% -> 0%
where the time goes in v1:
time: 22 us; the launch traced here: 21.8 us
  Pallas kernels  17.1 us (78%)
  between operations  2.4 us (11%)
  local copies, waits for them, and re-layouts  2.29 us (10%)
    pallas_call x1, Pallas kernels, per_device(): pl.pallas_call(functools.partial(kernel, sizes), out_shape=(jax.ShapeDtyp...  17.1 us
    unnamed x4, local copies, waits for them, and re-layouts  2.29 us

profile of v1, /device:TPU:0, one launch (start us, length us, event | category | flops | bytes accessed | tf_op | source)
XLA Modules:
  0.0 21.8 jit_solution(5707991090484442562)
XLA Ops:
  0.6 17.1 %chebyshev.1 = (f32[152,256]{1,0:T(8,128)}, f32[152,256]{1,0:T(8,128)}, f32[1,1]{1,0:T(1,128)}) custom-call(f32[152,256]{1,0:T(8,128)} %f_in.1, f32[152,256]{1,0:T(8,128)} %g_in.1, f32[152,256]{1,0:T(8,128)} %s_in.1, s32[152,256]{1,0:T(8,128)} %m_in.1), custom_call_target="tpu_custom_call" | custom-call | tf_op jit(solution)/shard_map/chebyshev/pallas_call | solution.py:359
  17.8 0.0 copy-start
  17.8 1.6 %copy.10 = f32[152,256]{1,0:T(8,128)} copy(f32[152,256]{1,0:T(8,128)} %get-tuple-element.12) | data formatting | bytes 311296
  19.4 0.0 copy-done
  19.4 0.7 %copy.11 = f32[152,256]{1,0:T(8,128)} copy(f32[152,256]{1,0:T(8,128)S(1)} %copy-done) | data formatting | bytes 311296
Async XLA Ops:
  17.8 1.6 %copy-start = (f32[152,256]{1,0:T(8,128)S(1)}, f32[152,256]{1,0:T(8,128)}, u32[]{:S(2)}) copy-start(f32[152,256]{1,0:T(8,128)} %get-tuple-element.13) | copy-start | bytes 466948

commit v2 on v1

--- a/solution.py
+++ b/solution.py
@@ -52,9 +52,9 @@
 def kernel(
     sizes,
     f_in, g_in, s_in, m_in,
-    x_out, r_out, norm_out,
-    ext, ext_m, mask, flip_f, flip_m, pack, came, corner, flip_c, x_buf, r_buf, part, parts,
-    load_sem, send_sem, recv_sem, part_send, part_recv, own_sem, out_sem,
+    x_buf, r_buf, norm_out,
+    ext, ext_m, mask, flip_f, flip_m, pack, came, corner, flip_c, part, parts,
+    load_sem, send_sem, recv_sem, part_send, part_recv,
 ):
     nbx, nby, rows, cols = sizes
     n = nbx * nby
@@ -178,24 +178,34 @@
 
     @pl.when(jnp.logical_not(bottom))
     def _():
-        for copy in to_south:
+        for copy in to_south[:2]:
             copy.start()
 
     @pl.when(jnp.logical_not(fold))
     def _():
-        for copy in to_north:
+        for copy in to_north[:2]:
             copy.start()
 
+    to_west.start()
+    to_east.start()
+
+    @pl.when(jnp.logical_not(bottom))
+    def _():
+        for copy in to_south[2:]:
+            copy.start()
+
+    @pl.when(jnp.logical_not(fold))
+    def _():
+        for copy in to_north[2:]:
+            copy.start()
+
     @pl.when(fold)
     def _():
+        for copy in over_fold:
+            copy.start()
         for remote, local, target in fold_corners:
             pl.when(target != bx)(remote.start)
             pl.when(target == bx)(local.start)
-        for copy in over_fold:
-            copy.start()
-
-    to_west.start()
-    to_east.start()
 
     to_west.wait_recv()
     to_east.wait_recv()
@@ -282,10 +292,6 @@
     final = resid[low:high, :cols]
     x_buf[...] = iterate[low:high, :cols]
     r_buf[...] = final
-    out_x = pltpu.make_async_copy(x_buf, x_out, out_sem.at[0])
-    out_r = pltpu.make_async_copy(r_buf, r_out, out_sem.at[1])
-    out_x.start()
-    out_r.start()
 
     square = final * final
     row_sums = jnp.sum(square, axis=1, keepdims=True)
@@ -299,7 +305,7 @@
     def share(k):
         other = lax.rem(me + k, n)
         return pltpu.make_async_remote_copy(
-            src_ref=part, dst_ref=parts.at[me], send_sem=part_send.at[k], recv_sem=part_recv.at[me],
+            src_ref=part, dst_ref=parts.at[me], send_sem=part_send.at[0], recv_sem=part_recv.at[0],
             device_id=(other // nby, lax.rem(other, nby)), device_id_type=MESH_ID,
         )
 
@@ -330,13 +336,9 @@
         for copy in over_fold:
             copy.wait_send()
 
-    def finish(k, carry):
-        share(k).wait_send()
-        source = lax.rem(me + k, n)
-        pltpu.make_async_copy(part, parts.at[source], part_recv.at[source]).wait()
-        return carry
-
-    lax.fori_loop(1, n, finish, 0)
+    others = parts.at[pl.ds(0, n - 1)]
+    pltpu.make_async_copy(others, others, part_send.at[0]).wait()
+    pltpu.make_async_copy(others, others, part_recv.at[0]).wait()
 
     def words(i):
         row = parts[i]
@@ -344,8 +346,17 @@
 
     upper, lower = pair_tree([words(i) for i in range(n)])
     norm_out[...] = jnp.sqrt((upper + lower) / (rows * cols * n))[:, 0:1]
-    out_x.wait()
-    out_r.wait()
+
+
+def write_out(x_in, r_in, x_out, r_out, sem):
+    copies = [
+        pltpu.make_async_copy(x_in, x_out, sem.at[0]),
+        pltpu.make_async_copy(r_in, r_out, sem.at[1]),
+    ]
+    for copy in copies:
+        copy.start()
+    for copy in copies:
+        copy.wait()
 
 
 def per_device(sizes, forcing, guess, shift, ocean_mask):
@@ -356,15 +367,16 @@
     pack_rows = 8 * -(-(rows // 8) // chunks)
     f32 = jnp.float32
     hbm = pl.BlockSpec(memory_space=pl.ANY)
+    vmem = pl.BlockSpec(memory_space=pltpu.VMEM)
     x, r, norm = pl.pallas_call(
         functools.partial(kernel, sizes),
         out_shape=(
-            jax.ShapeDtypeStruct((rows, cols), f32),
-            jax.ShapeDtypeStruct((rows, cols), f32),
+            pltpu.VMEM((rows, cols), f32),
+            pltpu.VMEM((rows, cols), f32),
             jax.ShapeDtypeStruct((1, 1), f32),
         ),
         in_specs=[hbm] * 4,
-        out_specs=(hbm, hbm, pl.BlockSpec(memory_space=pltpu.VMEM)),
+        out_specs=(vmem, vmem, vmem),
         scratch_shapes=[
             pltpu.VMEM((3, whole, width), f32),
             pltpu.VMEM((whole, cols), jnp.int32),
@@ -375,21 +387,28 @@
             pltpu.VMEM((2, pack_rows, LANES), f32),
             pltpu.VMEM((4, 8, LANES), f32),
             pltpu.VMEM((2, 8, LANES), f32),
-            pltpu.VMEM((rows, cols), f32),
-            pltpu.VMEM((rows, cols), f32),
             pltpu.VMEM((1, LANES), f32),
             pltpu.VMEM((n, 1, LANES), f32),
             pltpu.SemaphoreType.DMA((4,)),
             pltpu.SemaphoreType.DMA((10,)),
             pltpu.SemaphoreType.DMA((10,)),
-            pltpu.SemaphoreType.DMA((n,)),
-            pltpu.SemaphoreType.DMA((n,)),
             pltpu.SemaphoreType.DMA((1,)),
-            pltpu.SemaphoreType.DMA((2,)),
+            pltpu.SemaphoreType.DMA((1,)),
         ],
         compiler_params=pltpu.CompilerParams(collective_id=0, has_side_effects=True),
         name="chebyshev",
     )(forcing, guess, shift, ocean_mask)
+    x = pltpu.with_memory_space_constraint(x, pltpu.VMEM)
+    r = pltpu.with_memory_space_constraint(r, pltpu.VMEM)
+    field = jax.ShapeDtypeStruct((rows, cols), f32)
+    x, r = pl.pallas_call(
+        write_out,
+        out_shape=(field, field),
+        in_specs=[hbm] * 2,
+        out_specs=(hbm, hbm),
+        scratch_shapes=[pltpu.SemaphoreType.DMA((2,))],
+        name="write_out",
+    )(x, r)
     return x, r, norm.reshape(())
 
 

time: 22 us -> 19.9 us (0.905)
  local copies, waits for them, and re-layouts: 2.29 us -> 0 us
    unnamed x4 -> x0, local copies, waits for them, and re-layouts: 2.29 us -> none
    pallas_call x1 -> x2, Pallas kernels: 17.1 us -> 17.3 us  [the longest x1 16.6 us: per_device(): pl.pallas_call(functools.partial(kernel, sizes), out_shape=(pltpu.VMEM((r...]
where the time goes in v2:
time: 19.9 us; the launch traced here: 19.7 us
  Pallas kernels  17.3 us (87%)
  between operations  2.4 us (12%)
    pallas_call x1, Pallas kernels, per_device(): pl.pallas_call(functools.partial(kernel, sizes), out_shape=(pltpu.VMEM((r...  16.6 us
    pallas_call x1, Pallas kernels, per_device(): pl.pallas_call(write_out, out_shape=(field, field), in_specs=[hbm] * 2, o...  0.73 us

profile of v2, /device:TPU:0, one launch (start us, length us, event | category | flops | bytes accessed | tf_op | source)
XLA Modules:
  0.0 19.7 jit_solution(14403038527323734409)
XLA Ops:
  0.6 16.6 %chebyshev.1 = (f32[152,256]{1,0:T(8,128)S(1)}, f32[152,256]{1,0:T(8,128)S(1)}, f32[1,1]{1,0:T(1,128)}) custom-call(f32[152,256]{1,0:T(8,128)} %f_in.1, f32[152,256]{1,0:T(8,128)} %g_in.1, f32[152,256]{1,0:T(8,128)} %s_in.1, s32[152,256]{1,0:T(8,128)} %m_in.1), custom_call_target="tpu_custom_call" | custom-call | tf_op jit(solution)/shard_map/chebyshev/pallas_call | solution.py:371
  17.2 0.7 %write_out.1 = (f32[152,256]{1,0:T(8,128)}, f32[152,256]{1,0:T(8,128)}) custom-call(f32[152,256]{1,0:T(8,128)S(1)} %get-tuple-element.8.x_in, f32[152,256]{1,0:T(8,128)S(1)} %get-tuple-element.9.r_in), custom_call_target="tpu_custom_call" | custom-call | tf_op jit(solution)/shard_map/write_out/pallas_call | solution.py:404

commit v3 on v2

--- a/solution.py
+++ b/solution.py
@@ -47,6 +47,16 @@
 def turn(tile, shift):
     shift = shift % LANES
     return tile if shift == 0 else pltpu.roll(tile, shift, 1)
+
+
+def other_devices(bx, by, nbx, nby):
+    order = sorted(range(nby), key=lambda k: -min(k, nby - k))
+    return [
+        (lax.rem(bx + i, nbx), lax.rem(by + k, nby))
+        for k in order
+        for i in reversed(range(nbx))
+        if i or k
+    ]
 
 
 def kernel(
@@ -72,6 +82,11 @@
     top = pl.ds(8 * top_slot, 8)
     lane = lax.broadcasted_iota(jnp.int32, (8, LANES), 1)
 
+    barrier = pltpu.get_barrier_semaphore()
+    others = other_devices(bx, by, nbx, nby)
+    for other in others:
+        pl.semaphore_signal(barrier, inc=1, device_id=other, device_id_type=MESH_ID)
+
     loads = [
         pltpu.make_async_copy(source, ext.at[k, pl.ds(low, rows), pl.ds(0, cols)], load_sem.at[k])
         for k, source in enumerate((f_in, g_in, s_in))
@@ -79,17 +94,6 @@
     loads.append(pltpu.make_async_copy(m_in, ext_m.at[pl.ds(low, rows), :], load_sem.at[3]))
     for copy in loads:
         copy.start()
-
-    barrier = pltpu.get_barrier_semaphore()
-
-    def greet(k, carry):
-        other = lax.rem(me + k, n)
-        pl.semaphore_signal(
-            barrier, inc=1, device_id=(other // nby, lax.rem(other, nby)), device_id_type=MESH_ID
-        )
-        return carry
-
-    lax.fori_loop(1, n, greet, 0)
 
     for copy in loads:
         copy.wait()
@@ -302,18 +306,11 @@
         pair = pair_add(pair, [pltpu.roll(word, step, 0) for word in pair])
     part[...] = jnp.where(lane < LANES // 2, pair[0], pair[1])[0:1]
 
-    def share(k):
-        other = lax.rem(me + k, n)
-        return pltpu.make_async_remote_copy(
+    for other in others:
+        pltpu.make_async_remote_copy(
             src_ref=part, dst_ref=parts.at[me], send_sem=part_send.at[0], recv_sem=part_recv.at[0],
-            device_id=(other // nby, lax.rem(other, nby)), device_id_type=MESH_ID,
-        )
-
-    def begin(k, carry):
-        share(k).start()
-        return carry
-
-    lax.fori_loop(1, n, begin, 0)
+            device_id=other, device_id_type=MESH_ID,
+        ).start()
     parts[me] = part[...]
 
     to_west.wait_send()
@@ -336,22 +333,25 @@
         for copy in over_fold:
             copy.wait_send()
 
-    others = parts.at[pl.ds(0, n - 1)]
-    pltpu.make_async_copy(others, others, part_send.at[0]).wait()
-    pltpu.make_async_copy(others, others, part_recv.at[0]).wait()
+    bulk = parts.at[pl.ds(0, n - 1)]
+    pltpu.make_async_copy(bulk, bulk, part_send.at[0]).wait()
+    pltpu.make_async_copy(bulk, bulk, part_recv.at[0]).wait()
 
     def words(i):
         row = parts[i]
         return row, pltpu.roll(row, LANES // 2, 1)
 
     upper, lower = pair_tree([words(i) for i in range(n)])
-    norm_out[...] = jnp.sqrt((upper + lower) / (rows * cols * n))[:, 0:1]
-
-
-def write_out(x_in, r_in, x_out, r_out, sem):
+    norm = jnp.sqrt((upper + lower) / (rows * cols * n))
+    norm_out[...] = jnp.broadcast_to(norm, norm_out.shape)
+
+
+def write_out(x_in, r_in, norm_in, x_out, r_out, norm_out, word, sem):
+    word[...] = norm_in[0:1, 0:1]
     copies = [
         pltpu.make_async_copy(x_in, x_out, sem.at[0]),
         pltpu.make_async_copy(r_in, r_out, sem.at[1]),
+        pltpu.make_async_copy(word, norm_out, sem.at[2]),
     ]
     for copy in copies:
         copy.start()
@@ -373,7 +373,7 @@
         out_shape=(
             pltpu.VMEM((rows, cols), f32),
             pltpu.VMEM((rows, cols), f32),
-            jax.ShapeDtypeStruct((1, 1), f32),
+            pltpu.VMEM((8, LANES), f32),
         ),
         in_specs=[hbm] * 4,
         out_specs=(vmem, vmem, vmem),
@@ -400,15 +400,16 @@
     )(forcing, guess, shift, ocean_mask)
     x = pltpu.with_memory_space_constraint(x, pltpu.VMEM)
     r = pltpu.with_memory_space_constraint(r, pltpu.VMEM)
+    norm = pltpu.with_memory_space_constraint(norm, pltpu.VMEM)
     field = jax.ShapeDtypeStruct((rows, cols), f32)
-    x, r = pl.pallas_call(
+    x, r, norm = pl.pallas_call(
         write_out,
-        out_shape=(field, field),
-        in_specs=[hbm] * 2,
-        out_specs=(hbm, hbm),
-        scratch_shapes=[pltpu.SemaphoreType.DMA((2,))],
+        out_shape=(field, field, jax.ShapeDtypeStruct((1, 1), f32)),
+        in_specs=[hbm, hbm, vmem],
+        out_specs=(hbm,) * 3,
+        scratch_shapes=[pltpu.VMEM((1, 1), f32), pltpu.SemaphoreType.DMA((3,))],
         name="write_out",
-    )(x, r)
+    )(x, r, norm)
     return x, r, norm.reshape(())
 
 

time: 19.9 us -> 17.6 us (0.88)
  between operations: 2.4 us -> 0.64 us
  Pallas kernels: 17.3 us -> 16.8 us
    pallas_call x1, Pallas kernels: 16.6 us -> 16 us  [per_device(): pl.pallas_call(functools.partial(kernel, sizes), out_shape=(pltpu.VMEM((r...]
where the time goes in v3:
time: 17.6 us; the launch traced here: 17.4 us
  Pallas kernels  16.8 us (95%)
  between operations  0.64 us (4%)
    pallas_call x1, Pallas kernels, per_device(): pl.pallas_call(functools.partial(kernel, sizes), out_shape=(pltpu.VMEM((r...  16 us
    pallas_call x1, Pallas kernels, per_device(): pl.pallas_call(write_out, out_shape=(field, field, jax.ShapeDtypeStruct((...  0.75 us

profile of v3, /device:TPU:0, one launch (start us, length us, event | category | flops | bytes accessed | tf_op | source)
XLA Modules:
  0.0 17.4 jit_solution(14257457007726500867)
XLA Ops:
  0.6 16.0 %chebyshev.1 = (f32[152,256]{1,0:T(8,128)S(1)}, f32[152,256]{1,0:T(8,128)S(1)}, f32[8,128]{1,0:T(8,128)S(1)}) custom-call(f32[152,256]{1,0:T(8,128)} %f_in.1, f32[152,256]{1,0:T(8,128)} %g_in.1, f32[152,256]{1,0:T(8,128)} %s_in.1, s32[152,256]{1,0:T(8,128)} %m_in.1), custom_call_target="tpu_custom_call" | custom-call | tf_op jit(solution)/shard_map/chebyshev/pallas_call | solution.py:371
  16.7 0.7 %write_out.1 = (f32[152,256]{1,0:T(8,128)}, f32[152,256]{1,0:T(8,128)}, f32[1,1]{1,0:T(1,128)}) custom-call(f32[152,256]{1,0:T(8,128)S(1)} %get-tuple-element.9.x_in, f32[152,256]{1,0:T(8,128)S(1)} %get-tuple-element.10.r_in, f32[8,128]{1,0:T(8,128)S(1)} %get-tuple-element.11.norm_in), custom_call_target="tpu_custom_call" | custom-call | tf_op jit(solution)/shard_map/write_out/pallas_call | solution.py:405
